TPU v7x, 32 devices: a whole 2x2x4 slice. The times are simulated.
32 devices in a mesh: row: 4 (over z), col: 8 (over y, x, core).
Axes of the slice: x: 2, y: 2, z: 4, core: 2. Of those that a mesh axis runs over, the one named last changes fastest.
Arguments:
- tokens: bfloat16 [24576, 256], P(('row', 'col'))
- codebook: bfloat16 [16384, 256], P(('row', 'col')), may hold values from -6 to 6
- codes: int32 [24576], P(('row', 'col')), may hold values from 0 to 16383
Outputs:
- quantized: bfloat16 [24576, 256], P(('row', 'col'))
- token_loss: float32 [24576], P(('row', 'col'))
- code_counts: int32 [16384], P(('row', 'col'))
- code_loss: float32 [16384], P(('row', 'col'))
- commitment: float32 [], replicated
- perplexity: float32 [], replicated
All inputs are finite; a program needn't handle non-finite values.
Results may differ from a plain program's by a relative error of at most 0.0004.
Values may be sent and summed in bfloat16 or wider, within the bound.
A program may use at most 64 MiB of HBM per device.

v0:
```python
import jax
import jax.numpy as jnp
from jax import lax
from jax.sharding import PartitionSpec as P


def on_device(tokens, codebook, codes):
    tok_rows = tokens.shape[0]
    width = tokens.shape[1]
    per_dev = codebook.shape[0]
    devices = lax.axis_size("row") * lax.axis_size("col")
    total_codes = per_dev * devices
    total_tokens = tok_rows * devices
    full_book = lax.all_gather(codebook, ("row", "col"), axis=0, tiled=True)
    quantized = jnp.take(full_book, codes, axis=0)
    diff = tokens.astype(jnp.float32) - quantized.astype(jnp.float32)
    token_loss = jnp.sum(diff * diff, axis=1) / width
    loss_part = jnp.sum(token_loss)
    local_counts = jax.ops.segment_sum(
        jnp.ones((tok_rows,), jnp.float32), codes, num_segments=total_codes
    )
    local_loss = jax.ops.segment_sum(token_loss, codes, num_segments=total_codes)
    floor_prob = jnp.float32(1.0 / total_tokens)
    totals, loss_totals = lax.psum((local_counts, local_loss), ("row", "col"))
    loss_sum = lax.psum(loss_part, ("row", "col"))
    probs = totals / total_tokens
    terms = jnp.where(
        totals > 0.5, probs * jnp.log(jnp.maximum(probs, floor_prob)), jnp.float32(0.0)
    )
    entropy = jnp.sum(terms)
    offset = lax.axis_index(("row", "col")) * per_dev
    owned_counts = lax.dynamic_slice_in_dim(totals, offset, per_dev, 0)
    code_loss = lax.dynamic_slice_in_dim(loss_totals, offset, per_dev, 0)
    code_counts = owned_counts.astype(jnp.int32)
    commitment = 0.25 * loss_sum / total_tokens
    perplexity = jnp.exp(-entropy)
    return (quantized, token_loss, code_counts, code_loss, commitment, perplexity)


def solution(mesh):
    return jax.shard_map(
        on_device,
        mesh=mesh,
        in_specs=(P(("row", "col"), None), P(("row", "col"), None), P(("row", "col"))),
        out_specs=(
            P(("row", "col"), None),
            P(("row", "col")),
            P(("row", "col")),
            P(("row", "col")),
            P(),
            P(),
        ),
        check_vma=False,
    )
```

profile of v0, /device:TPU:0, one launch (start us, length us, event | category | flops | bytes accessed | tf_op | source)
XLA Modules:
  0.0 242.7 jit_solution(13343456410854663029)
XLA Ops:
  7.2 0.0 all-gather.2.cloned.1.call-start
  7.2 0.7 all-gather.2.cloned.1.call-update
  7.9 0.0 all-reduce.3.cloned.1.call-start
  8.0 5.3 %scatter_custom_fusion = f32[16384]{0:T(1024)} fusion(s32[768]{0:T(1024)} %param.5, f32[768]{0:T(1024)S(1)} %broadcast.9, f32[]{:T(128)} %constant.18.clone.1), kind=kCustom, calls=%fused_computation.8 | custom fusion | flops 768 | bytes 66048 | tf_op jit(solution)/shard_map/scatter-add | solution.py:19
  13.3 0.7 compare_select_fusion
  14.0 0.7 compare_and_fusion
  14.7 76.0 %all-gather.2.cloned.1.call-done = bf16[16384,256]{1,0:T(8,128)(2,1)} async-done(((bf16[512,256]{1,0:T(8,128)(2,1)}), bf16[16384,256]{1,0:T(8,128)(2,1)}) %all-gather.2.cloned.1.call-update) | async-done | bytes 8388624 | tf_op jit(solution)/shard_map/all_gather | solution.py:14
  90.6 6.6 %gather_fusion = bf16[768,256]{1,0:T(8,128)(2,1)S(1)} fusion(bf16[16384,256]{1,0:T(8,128)(2,1)} %all-gather.2.cloned.1.call-done, s32[1024]{0:T(1024)S(1)} %pad_clamp_fusion), kind=kCustom, calls=%fused_computation | custom fusion | bytes 789504 | tf_op jit(solution)/shard_map/jit(_take)/gather | solution.py:15
  97.2 2.0 multiply_reduce_fusion
  99.2 0.6 fusion.4
  99.8 0.0 copy-start
  99.8 5.3 %scatter_custom_fusion.1 = f32[16384]{0:T(1024)} fusion(s32[768]{0:T(1024)} %param.5, f32[768]{0:T(1024)S(1)} %get-tuple-element.9, f32[]{:T(128)} %constant.18.clone.1), kind=kCustom, calls=%fused_computation.6 | custom fusion | flops 768 | bytes 66048 | tf_op jit(solution)/shard_map/scatter-add | solution.py:22
  105.1 0.0 all-reduce.3.cloned.1.call-update
  105.1 39.6 %psum.23 = f32[]{:T(128)} all-reduce(f32[]{:T(128)} %get-tuple-element.8), channel_id=1, replica_groups=mesh['row'=4,'col'=8] {'row','col'}, use_global_device_ids=true, to_apply=%region_6.7 | all-reduce | flops 1 | bytes 8 | tf_op jit(solution)/shard_map/psum | solution.py:25
  145.4 83.4 %all-reduce.3.cloned.1.call-done = (f32[16384]{0:T(1024)}, f32[16384]{0:T(1024)}) async-done(((f32[16384]{0:T(1024)}, f32[16384]{0:T(1024)}), (f32[16384]{0:T(1024)}, f32[16384]{0:T(1024)})) %all-reduce.3.cloned.1.call-update) | async-done | bytes 131088 | tf_op jit(solution)/shard_map/psum | solution.py:24
  228.8 1.5 select_reduce_fusion
  230.2 1.3 dynamic-slice_convert_fusion
  231.6 1.3 dynamic_slice.7
  233.6 0.0 copy-done
  (2 shorter events, 0.0 us)
Async XLA Ops:
  7.2 83.5 %all-gather.2.cloned.1.call-start = ((), (), s32[]{:S(2)}) async-start(), calls=%async_computation | async-start | bytes 8650752 | tf_op jit(solution)/shard_map/all_gather | solution.py:14
  7.9 220.9 %all-reduce.3.cloned.1.call-start = ((), (), s32[]{:S(2)}) async-start(), calls=%async_computation.1 | async-start | bytes 262144 | tf_op jit(solution)/shard_map/psum | solution.py:24
  99.8 133.8 %copy-start = (f32[768]{0:T(1024)}, f32[768]{0:T(1024)S(1)}, u32[]{:S(2)}) copy-start(f32[768]{0:T(1024)S(1)} %get-tuple-element.9) | copy-start | bytes 9220
Sparse Core Ops, SparseCore 0:
  10.8 79.7 all-gather.1
  105.2 123.4 all-reduce.2
where the time goes:
time: 243 us
  waiting for transfers between devices  160 us (66%)
  blocking collectives  39.6 us (16%)
  between operations  17.7 us (7%)
  other arithmetic  17.4 us (7%)
  local copies, waits for them, and re-layouts  7.89 us (3%)
    psum x1, waiting for transfers between devices, on_device(): totals, loss_totals = lax.psum((local_counts, local_loss), ('row', 'col'))  83.4 us
    all_gather x1, waiting for transfers between devices, on_device(): full_book = lax.all_gather(codebook, ('row', 'col'), axis=0, tiled=True)  76 us
    psum x1, blocking collectives, on_device(): loss_sum = lax.psum(loss_part, ('row', 'col'))  39.6 us
    gather x1, local copies, waits for them, and re-layouts, on_device(): quantized = jnp.take(full_book, codes, axis=0)  6.56 us
    scatter-add x1, other arithmetic, on_device(): jax.ops.segment_sum(jnp.ones((tok_rows,), jnp.float32), codes, num_segmen...  5.32 us
    scatter-add x1, other arithmetic, on_device(): jax.ops.segment_sum(token_loss, codes, num_segments=total_codes)  5.3 us
  transfers between devices with their start and end apart: 2, of which 2 were waited for; matrix products, arithmetic and copies ran while one was open for 3% of the time, Pallas kernels for 0%

commit v1 on v0

v1 whole, which is shorter than its diff:
```python
import functools
import math

import jax
import jax.numpy as jnp
from jax import lax
from jax.experimental import pallas as pl
from jax.experimental.pallas import tpu as pltpu
from jax.sharding import PartitionSpec as P

AXES = ("row", "col")
EXTRA = 128
F32 = jnp.float32
BF16 = jnp.bfloat16


def dense_plan(tokens, codebook, codes):
    tok_rows = tokens.shape[0]
    width = tokens.shape[1]
    per_dev = codebook.shape[0]
    devices = lax.axis_size("row") * lax.axis_size("col")
    total_codes = per_dev * devices
    total_tokens = tok_rows * devices
    full_book = lax.all_gather(codebook, AXES, axis=0, tiled=True)
    quantized = jnp.take(full_book, codes, axis=0)
    diff = tokens.astype(F32) - quantized.astype(F32)
    token_loss = jnp.sum(diff * diff, axis=1) / width
    loss_part = jnp.sum(token_loss)
    local_counts = jax.ops.segment_sum(
        jnp.ones((tok_rows,), F32), codes, num_segments=total_codes
    )
    local_loss = jax.ops.segment_sum(token_loss, codes, num_segments=total_codes)
    floor_prob = jnp.float32(1.0 / total_tokens)
    totals, loss_totals = lax.psum((local_counts, local_loss), AXES)
    loss_sum = lax.psum(loss_part, AXES)
    probs = totals / total_tokens
    terms = jnp.where(
        totals > 0.5, probs * jnp.log(jnp.maximum(probs, floor_prob)), jnp.float32(0.0)
    )
    offset = lax.axis_index(AXES) * per_dev
    owned_counts = lax.dynamic_slice_in_dim(totals, offset, per_dev, 0)
    code_loss = lax.dynamic_slice_in_dim(loss_totals, offset, per_dev, 0)
    commitment = 0.25 * loss_sum / total_tokens
    return (
        quantized,
        token_loss,
        owned_counts.astype(jnp.int32),
        code_loss,
        commitment,
        jnp.exp(-jnp.sum(terms)),
    )


def ring_plan(n, tokens, codebook, codes):
    rows, width = tokens.shape
    per_dev = codebook.shape[0]
    me = lax.axis_index(AXES)
    ring = [(i, (i + 1) % n) for i in range(n)]
    hi = codes // per_dev
    lo = codes % per_dev

    def pick(step, carry):
        block, got = carry
        owner = lax.rem(me - step + n, n)
        got = jnp.where((hi == owner)[:, None], jnp.take(block, lo, axis=0), got)
        return lax.ppermute(block, AXES, ring), got

    _, quantized = lax.fori_loop(0, n, pick, (codebook, jnp.zeros_like(tokens)))
    diff = tokens.astype(F32) - quantized.astype(F32)
    token_loss = jnp.sum(diff * diff, axis=1) / width

    def add(step, carry):
        c, t, total, parts = carry
        owner = lax.rem(me - step + n, n)
        mine = (c // per_dev) == me
        total = total + jax.ops.segment_sum(
            jnp.where(mine, t, 0.0), c % per_dev, num_segments=per_dev
        )
        parts = lax.dynamic_update_slice(parts, jnp.sum(t)[None], (owner,))
        return lax.ppermute(c, AXES, ring), lax.ppermute(t, AXES, ring), total, parts

    start = (codes, token_loss, jnp.zeros((per_dev,), F32), jnp.zeros((n,), F32))
    _, _, code_loss, parts = lax.fori_loop(0, n, add, start)
    return quantized, token_loss, code_loss, 0.25 * jnp.sum(parts) / (rows * n)


def kernel(
    n, cols, cap, stride,
    codes_ref, tokens_ref, book_ref,
    quant_ref, tloss_ref, counts_ref, closs_ref, commit_ref, perp_ref, flag_ref,
    csend, crecv, psend, precv, lsend, lrecv, ranks, low1h, sel,
    csem_s, csem_r, psem_s, psem_r, lsem_s, lsem_r,
):
    rows, width = tokens_ref.shape
    per = book_ref.shape[0]
    bits = per.bit_length() - 1
    total_tokens = rows * n
    me = lax.axis_index("row") * cols + lax.axis_index("col")

    def where_is(r):
        return (r // cols, lax.rem(r, cols))

    def peer(k):
        return lax.rem(me + lax.rem(k * stride, n), n)

    def copy(send, recv, ssem, rsem, r):
        return pltpu.make_async_remote_copy(
            src_ref=send.at[r],
            dst_ref=recv.at[me],
            send_sem=ssem.at[r],
            recv_sem=rsem.at[me],
            device_id=where_is(r),
            device_id_type=pl.DeviceIdType.MESH,
        )

    def arrived(send, recv, ssem, rsem, r):
        pltpu.make_async_remote_copy(
            src_ref=send.at[r],
            dst_ref=recv.at[r],
            send_sem=ssem.at[r],
            recv_sem=rsem.at[r],
            device_id=where_is(r),
            device_id_type=pl.DeviceIdType.MESH,
        ).wait_recv()

    def each_peer(fn):
        def body(k, _):
            fn(peer(k))
            return 0

        lax.fori_loop(1, n, body, 0)

    barrier = pltpu.get_barrier_semaphore()
    each_peer(
        lambda r: pl.semaphore_signal(
            barrier, inc=1, device_id=where_is(r), device_id_type=pl.DeviceIdType.MESH
        )
    )

    code_row = codes_ref[...]
    hi_row = lax.shift_right_logical(code_row, bits)
    code_col = jnp.broadcast_to(code_row.astype(F32), (128, rows)).T.astype(jnp.int32)
    hi_col = lax.shift_right_logical(code_col, bits)
    lo_col = code_col & (per - 1)
    lane = lax.broadcasted_iota(jnp.int32, (rows, 128), 1)
    own_row = hi_row == lax.broadcasted_iota(jnp.int32, (n, rows), 0)
    for k in range(per // 128):
        low1h[:, k * 128 : (k + 1) * 128] = jnp.where(lo_col == lane + k * 128, 1.0, 0.0).astype(BF16)
    low = low1h[...]
    hist = jnp.dot(jnp.where(own_row, 1.0, 0.0).astype(BF16), low, preferred_element_type=F32)
    wanted = jnp.where(hist > 0.5, 1.0, 0.0)
    most = jnp.max(jnp.sum(wanted, axis=1, keepdims=True), axis=0, keepdims=True)
    most_wide = jnp.broadcast_to(most, (1, EXTRA))
    for p in range(n):
        csend[p, :, :per] = hist[p : p + 1, :]
        csend[p, :, per:] = most_wide
    crecv[pl.ds(me, 1)] = csend[pl.ds(me, 1)]

    pl.semaphore_wait(barrier, n - 1)
    each_peer(lambda r: copy(csend, crecv, csem_s, csem_r, r).start())

    before = lax.broadcasted_iota(jnp.int32, (per, per), 0) < lax.broadcasted_iota(jnp.int32, (per, per), 1)
    before = jnp.where(before, 1.0, 0.0).astype(BF16)
    rank = jnp.dot(wanted.astype(BF16), before, preferred_element_type=F32)
    rank = jnp.minimum(rank, 255.0).astype(BF16)
    hi1h = jnp.where(hi_col[:, :n] == lane[:, :n], 1.0, 0.0).astype(BF16)
    looked = jnp.dot(hi1h, rank, preferred_element_type=F32).astype(BF16) * low
    found = jnp.dot(looked, jnp.ones((per, 128), BF16), preferred_element_type=F32)
    slot = hi_col * cap + found.astype(jnp.int32)
    for k in range(n * cap // 128):
        sel[:, k * 128 : (k + 1) * 128] = jnp.where(slot == lane + k * 128, 1.0, 0.0).astype(BF16)

    each_peer(lambda r: arrived(csend, crecv, csem_s, csem_r, r))
    asked = crecv[:, 0, :per]
    present = asked > 0.5
    order = jnp.dot(jnp.where(present, 1.0, 0.0).astype(BF16), before, preferred_element_type=F32)
    order = jnp.where(present, order, -1.0)
    for p in range(n):
        ranks[p] = order[p : p + 1, :]

    place = lax.broadcasted_iota(jnp.int32, (cap, per), 0).astype(F32)

    def pack(r):
        picks = jnp.where(jnp.broadcast_to(ranks[r], (cap, per)) == place, 1.0, 0.0).astype(BF16)
        return jnp.dot(picks, book_ref[...], preferred_element_type=F32).astype(BF16)

    def pack_and_send(k, _):
        r = peer(k)
        psend[r] = pack(r)

        @pl.when(k > 1)
        def _():
            copy(psend, precv, psem_s, psem_r, peer(k - 1)).start()

        return 0

    lax.fori_loop(1, n, pack_and_send, 0)
    precv[me] = pack(me)
    copy(psend, precv, psem_s, psem_r, peer(n - 1)).start()

    counts = jnp.sum(asked, axis=0, keepdims=True)
    counts_ref[...] = counts.astype(jnp.int32)
    probs = counts / total_tokens
    terms = jnp.where(
        counts > 0.5, probs * jnp.log(jnp.maximum(probs, 1.0 / total_tokens)), 0.0
    )
    entropy = jnp.sum(terms, axis=1, keepdims=True)
    flag_ref[0, 0] = jnp.max(crecv[:, 0, per:]).astype(jnp.int32)

    each_peer(lambda r: arrived(psend, precv, psem_s, psem_r, r))
    packs = precv[...].reshape(n * cap, width)
    quant = jnp.dot(sel[...], packs, preferred_element_type=F32).astype(BF16)
    quant_ref[...] = quant
    diff = tokens_ref[...].astype(F32) - quant.astype(F32)
    square = diff * diff
    folded = square[:, :128]
    for k in range(1, width // 128):
        folded = folded + square[:, k * 128 : (k + 1) * 128]
    tloss = jnp.sum(folded.T, axis=0, keepdims=True) / width
    tloss_ref[...] = tloss
    part = jnp.sum(tloss, axis=1, keepdims=True)

    first = tloss.astype(BF16).astype(F32)
    second = (tloss - first).astype(BF16).astype(F32)
    third = tloss - first - second
    spread = jnp.concatenate(
        [jnp.where(own_row, x, 0.0).astype(BF16) for x in (first, second, third)], axis=0
    )
    sums = jnp.dot(spread, low1h[...], preferred_element_type=F32)
    sums = sums[:n] + sums[n : 2 * n] + sums[2 * n :]
    lane1 = lax.broadcasted_iota(jnp.int32, (1, EXTRA), 1)
    tail = jnp.where(lane1 == 0, part, jnp.where(lane1 == 1, entropy, 0.0))
    for p in range(n):
        lsend[p, :, :per] = sums[p : p + 1, :]
        lsend[p, :, per:] = tail
    lrecv[pl.ds(me, 1)] = lsend[pl.ds(me, 1)]
    each_peer(lambda r: copy(lsend, lrecv, lsem_s, lsem_r, r).start())

    def sent(r):
        copy(csend, crecv, csem_s, csem_r, r).wait_send()
        copy(psend, precv, psem_s, psem_r, r).wait_send()

    each_peer(sent)
    each_peer(lambda r: arrived(lsend, lrecv, lsem_s, lsem_r, r))
    added = jnp.sum(lrecv[:, 0, :], axis=0, keepdims=True)
    closs_ref[...] = added[:, :per]
    ends = added[:, per:]
    commit_ref[0, 0] = jnp.sum(jnp.where(lane1 == 0, ends, 0.0)) * (0.25 / total_tokens)
    perp = jnp.exp(-jnp.sum(jnp.where(lane1 == 1, ends, 0.0), axis=1, keepdims=True))
    perp_ref[0, 0] = jnp.max(jnp.broadcast_to(perp, (1, EXTRA)))
    each_peer(lambda r: copy(lsend, lrecv, lsem_s, lsem_r, r).wait_send())


def asked_plan(n, cols, tokens, codebook, codes):
    rows, width = tokens.shape
    per = codebook.shape[0]
    cap = -(-2 * rows // (n * 16)) * 16
    stride = next(s for s in range(n // 3 + 1, 2 * n) if math.gcd(s, n) == 1)
    vmem = pl.BlockSpec(memory_space=pltpu.VMEM)
    smem = pl.BlockSpec(memory_space=pltpu.SMEM)
    dma = pltpu.SemaphoreType.DMA((n,))
    message = pltpu.VMEM((n, 1, per + EXTRA), F32)
    quantized, token_loss, counts, code_loss, commitment, perplexity, flag = pl.pallas_call(
        functools.partial(kernel, n, cols, cap, stride),
        out_shape=(
            jax.ShapeDtypeStruct((rows, width), BF16),
            jax.ShapeDtypeStruct((1, rows), F32),
            jax.ShapeDtypeStruct((1, per), jnp.int32),
            jax.ShapeDtypeStruct((1, per), F32),
            jax.ShapeDtypeStruct((1, 1), F32),
            jax.ShapeDtypeStruct((1, 1), F32),
            jax.ShapeDtypeStruct((1, 1), jnp.int32),
        ),
        in_specs=[vmem] * 3,
        out_specs=(vmem, vmem, vmem, vmem, smem, smem, smem),
        scratch_shapes=[
            message, message,
            pltpu.VMEM((n, cap, width), BF16),
            pltpu.VMEM((n, cap, width), BF16),
            message, message,
            pltpu.VMEM((n, 1, per), F32),
            pltpu.VMEM((rows, per), BF16),
            pltpu.VMEM((rows, n * cap), BF16),
            dma, dma, dma, dma, dma, dma,
        ],
        compiler_params=pltpu.CompilerParams(collective_id=0, has_side_effects=True),
    )(codes.reshape(1, rows), tokens, codebook)

    def kept():
        return quantized, token_loss.reshape(rows), code_loss.reshape(per), commitment[0, 0]

    quantized, token_loss, code_loss, commitment = lax.cond(
        flag[0, 0] > cap, lambda: ring_plan(n, tokens, codebook, codes), kept
    )
    return (
        quantized,
        token_loss,
        counts.reshape(per),
        code_loss,
        commitment,
        perplexity[0, 0],
    )


def on_device(n, cols, tokens, codebook, codes):
    rows, width = tokens.shape
    per = codebook.shape[0]
    cap = -(-2 * rows // (n * 16)) * 16
    fits = (
        per % 128 == 0
        and per & (per - 1) == 0
        and rows % 128 == 0
        and width % 128 == 0
        and n * cap % 128 == 0
        and n % 8 == 0
        and n <= 128
        and cap < min(per, 256)
    )
    if fits:
        return asked_plan(n, cols, tokens, codebook, codes)
    return dense_plan(tokens, codebook, codes)


def solution(mesh):
    n = mesh.shape["row"] * mesh.shape["col"]
    return jax.shard_map(
        functools.partial(on_device, n, mesh.shape["col"]),
        mesh=mesh,
        in_specs=(P(AXES, None), P(AXES, None), P(AXES)),
        out_specs=(P(AXES, None), P(AXES), P(AXES), P(AXES), P(), P()),
        check_vma=False,
    )
```

time: 243 us -> 51.5 us (0.21)
  waiting for transfers between devices: 160 us -> 0 us
  Pallas kernels: 0 us -> 41 us
  blocking collectives: 39.6 us -> 0 us
  other arithmetic: 17.4 us -> 0.02 us
  between operations: 17.7 us -> 4.71 us
  local copies, waits for them, and re-layouts: 7.89 us -> 5.43 us
    psum x1 -> x0, waiting for transfers between devices: 83.4 us -> none  [on_device(): totals, loss_totals = lax.psum((local_counts, local_loss), ('row', 'col'))]
    all_gather x1 -> x0, waiting for transfers between devices: 76 us -> none  [on_device(): full_book = lax.all_gather(codebook, ('row', 'col'), axis=0, tiled=True)]
    pallas_call x0 -> x1, Pallas kernels: none -> 41 us  [asked_plan(): pl.pallas_call(functools.partial(kernel, n, cols, cap, stride), out_shape...]
    psum x1 -> x0, blocking collectives: 39.6 us -> none  [on_device(): loss_sum = lax.psum(loss_part, ('row', 'col'))]
    scatter-add x2 -> x0, other arithmetic: 10.6 us -> none  [the longest x1 5.32 us: on_device(): jax.ops.segment_sum(jnp.ones((tok_rows,), jnp.float32), codes, num_segmen...]
    gather x1 -> x0, local copies, waits for them, and re-layouts: 6.56 us -> none  [on_device(): quantized = jnp.take(full_book, codes, axis=0)]
    unnamed x2 -> x11, local copies, waits for them, and re-layouts: 0.01 us -> 4.85 us
    reduce_sum x3 -> x0, other arithmetic: 4.07 us -> none  [the longest x1 2 us: on_device(): token_loss = jnp.sum(diff * diff, axis=1) / width]
  transfers between devices with their start and end apart: 2 -> 0, of which waited for: 2 -> 0; matrix products, arithmetic and copies ran while one was open for 3% -> 0% of each run, Pallas kernels for 0% -> 0%
where the time goes in v1:
time: 51.5 us; the launch traced here: 51.2 us
  Pallas kernels  41 us (80%)
  local copies, waits for them, and re-layouts  5.43 us (11%)
  between operations  4.71 us (9%)
    pallas_call x1, Pallas kernels, asked_plan(): pl.pallas_call(functools.partial(kernel, n, cols, cap, stride), out_shape...  41 us
    unnamed x11, local copies, waits for them, and re-layouts  4.85 us

profile of v1, /device:TPU:0, one launch (start us, length us, event | category | flops | bytes accessed | tf_op | source)
XLA Modules:
  0.0 51.2 jit_solution(8918662920040111127)
XLA Ops:
  0.6 0.0 copy-start.2
  0.6 0.7 %copy.51 = s32[768]{0:T(1024)S(1)} copy(s32[768]{0:T(1024)} %param.11) | data formatting | bytes 6144
  1.4 0.9 %copy.50.book_ref = bf16[512,256]{1,0:T(8,128)(2,1)S(1)} copy(bf16[512,256]{1,0:T(8,128)(2,1)} %param.10) | data formatting | bytes 524288
  2.3 0.6 %reshape.55.codes_ref = s32[1,768]{1,0:T(1,128)} reshape(s32[768]{0:T(1024)S(1)} %copy.51) | data formatting | bytes 6144 | tf_op jit(solution)/shard_map/reshape | solution.py:287
  2.9 0.0 copy-done.2
  2.9 41.0 %shard_map.82 = (bf16[768,256]{1,0:T(8,128)(2,1)S(1)}, f32[1,768]{1,0:T(1,128)S(1)}, s32[1,512]{1,0:T(1,128)}, f32[1,512]{1,0:T(1,128)}, f32[1,1]{1,0:T(1,128)}, /*index=5*/f32[1,1]{1,0:T(1,128)}, s32[1,1]{1,0:T(1,128)}) custom-call(s32[1,768]{1,0:T(1,128)} %reshape.55.codes_ref, bf16[768,256]{1,0:T(8,128)(2,1)S(1)} %copy-done.2, ...), custom_call_target="tpu_custom_call" | custom-call | tf_op jit(solution)/shard_map/pallas_call | solution.py:263
  44.6 0.0 copy-start.5
  44.6 0.6 %copy-done.5 = f32[768]{0:T(1024)} copy-done((f32[768]{0:T(1024)}, f32[768]{0:T(1024)S(1)}, u32[]{:S(2)}) %copy-start.5) | copy-done | bytes 3096
  45.2 0.0 copy-start.6
  45.2 0.7 %copy.52 = bf16[768,256]{1,0:T(8,128)(2,1)} copy(bf16[768,256]{1,0:T(8,128)(2,1)S(1)} %get-tuple-element.527) | data formatting | bytes 786432
  45.9 0.0 copy-done.6
  45.9 0.6 %copy.53 = s32[512]{0:T(512)} copy(s32[512]{0:T(512)S(1)} %bitcast.8) | data formatting | bytes 4096
  46.5 1.2 %copy.54 = f32[512]{0:T(512)} copy(f32[512]{0:T(512)} %get-tuple-element.530) | data formatting | bytes 4096
  (2 shorter events, 0.0 us)
Async XLA Ops:
  0.6 2.3 %copy-start.2 = (bf16[768,256]{1,0:T(8,128)(2,1)S(1)}, bf16[768,256]{1,0:T(8,128)(2,1)}, u32[]{:S(2)}) copy-start(bf16[768,256]{1,0:T(8,128)(2,1)} %tokens_ref.1) | copy-start | bytes 1179652
  44.6 0.6 %copy-start.5 = (f32[768]{0:T(1024)}, f32[768]{0:T(1024)S(1)}, u32[]{:S(2)}) copy-start(f32[768]{0:T(1024)S(1)} %get-tuple-element.528) | copy-start | bytes 9220
  45.2 0.8 %copy-start.6 = (s32[1,512]{1,0:T(1,128)S(1)}, s32[1,512]{1,0:T(1,128)}, u32[]{:S(2)}) copy-start(s32[1,512]{1,0:T(1,128)} %get-tuple-element.312) | copy-start | bytes 6148

commit v2 on v1

--- a/solution.py
+++ b/solution.py
@@ -1,5 +1,4 @@
 import functools
-import math
 
 import jax
 import jax.numpy as jnp
@@ -10,6 +9,7 @@
 
 AXES = ("row", "col")
 EXTRA = 128
+GROUP = 4
 F32 = jnp.float32
 BF16 = jnp.bfloat16
 
@@ -85,7 +85,7 @@
 
 
 def kernel(
-    n, cols, cap, stride,
+    n, cols, cap, order_of,
     codes_ref, tokens_ref, book_ref,
     quant_ref, tloss_ref, counts_ref, closs_ref, commit_ref, perp_ref, flag_ref,
     csend, crecv, psend, precv, lsend, lrecv, ranks, low1h, sel,
@@ -95,47 +95,44 @@
     per = book_ref.shape[0]
     bits = per.bit_length() - 1
     total_tokens = rows * n
-    me = lax.axis_index("row") * cols + lax.axis_index("col")
-
-    def where_is(r):
-        return (r // cols, lax.rem(r, cols))
-
-    def peer(k):
-        return lax.rem(me + lax.rem(k * stride, n), n)
-
-    def copy(send, recv, ssem, rsem, r):
+    my_row, my_col = lax.axis_index("row"), lax.axis_index("col")
+    me = my_row * cols + my_col
+    rows_at = [lax.rem(my_row + d, n // cols) for d in range(n // cols)]
+    cols_at = [lax.rem(my_col + d, cols) for d in range(cols)]
+    at = [(rows_at[k // cols], cols_at[k % cols]) for k in range(n)]
+    peer = [r * cols + c for r, c in at]
+
+    def copy(send, recv, ssem, rsem, k):
         return pltpu.make_async_remote_copy(
-            src_ref=send.at[r],
+            src_ref=send.at[peer[k]],
             dst_ref=recv.at[me],
-            send_sem=ssem.at[r],
-            recv_sem=rsem.at[me],
-            device_id=where_is(r),
+            send_sem=ssem.at[k],
+            recv_sem=rsem.at[k],
+            device_id=at[k],
             device_id_type=pl.DeviceIdType.MESH,
         )
 
-    def arrived(send, recv, ssem, rsem, r):
-        pltpu.make_async_remote_copy(
-            src_ref=send.at[r],
-            dst_ref=recv.at[r],
-            send_sem=ssem.at[r],
-            recv_sem=rsem.at[r],
-            device_id=where_is(r),
-            device_id_type=pl.DeviceIdType.MESH,
-        ).wait_recv()
-
-    def each_peer(fn):
-        def body(k, _):
-            fn(peer(k))
-            return 0
-
-        lax.fori_loop(1, n, body, 0)
+    def start_all(*refs):
+        for k in order_of:
+            if k:
+                copy(*refs, k).start()
+
+    def wait_all(*refs):
+        for k in order_of:
+            if k:
+                copy(*refs, k).wait_recv()
+
+    def sent_all(*refs):
+        for k in order_of:
+            if k:
+                copy(*refs, k).wait_send()
 
     barrier = pltpu.get_barrier_semaphore()
-    each_peer(
-        lambda r: pl.semaphore_signal(
-            barrier, inc=1, device_id=where_is(r), device_id_type=pl.DeviceIdType.MESH
-        )
-    )
+    for k in order_of:
+        if k:
+            pl.semaphore_signal(
+                barrier, inc=1, device_id=at[k], device_id_type=pl.DeviceIdType.MESH
+            )
 
     code_row = codes_ref[...]
     hi_row = lax.shift_right_logical(code_row, bits)
@@ -157,7 +154,7 @@
     crecv[pl.ds(me, 1)] = csend[pl.ds(me, 1)]
 
     pl.semaphore_wait(barrier, n - 1)
-    each_peer(lambda r: copy(csend, crecv, csem_s, csem_r, r).start())
+    start_all(csend, crecv, csem_s, csem_r)
 
     before = lax.broadcasted_iota(jnp.int32, (per, per), 0) < lax.broadcasted_iota(jnp.int32, (per, per), 1)
     before = jnp.where(before, 1.0, 0.0).astype(BF16)
@@ -170,7 +167,7 @@
     for k in range(n * cap // 128):
         sel[:, k * 128 : (k + 1) * 128] = jnp.where(slot == lane + k * 128, 1.0, 0.0).astype(BF16)
 
-    each_peer(lambda r: arrived(csend, crecv, csem_s, csem_r, r))
+    wait_all(csend, crecv, csem_s, csem_r)
     asked = crecv[:, 0, :per]
     present = asked > 0.5
     order = jnp.dot(jnp.where(present, 1.0, 0.0).astype(BF16), before, preferred_element_type=F32)
@@ -179,24 +176,24 @@
         ranks[p] = order[p : p + 1, :]
 
     place = lax.broadcasted_iota(jnp.int32, (cap, per), 0).astype(F32)
-
-    def pack(r):
-        picks = jnp.where(jnp.broadcast_to(ranks[r], (cap, per)) == place, 1.0, 0.0).astype(BF16)
-        return jnp.dot(picks, book_ref[...], preferred_element_type=F32).astype(BF16)
-
-    def pack_and_send(k, _):
-        r = peer(k)
-        psend[r] = pack(r)
-
-        @pl.when(k > 1)
-        def _():
-            copy(psend, precv, psem_s, psem_r, peer(k - 1)).start()
-
-        return 0
-
-    lax.fori_loop(1, n, pack_and_send, 0)
-    precv[me] = pack(me)
-    copy(psend, precv, psem_s, psem_r, peer(n - 1)).start()
+    book = book_ref[...]
+    ready = []
+    for g in range(0, n, GROUP):
+        group = order_of[g : g + GROUP]
+        picks = [
+            jnp.where(jnp.broadcast_to(ranks[peer[k]], (cap, per)) == place, 1.0, 0.0).astype(BF16)
+            for k in group
+        ]
+        packed = jnp.dot(jnp.concatenate(picks, axis=0), book, preferred_element_type=F32)
+        packed = packed.astype(BF16)
+        for i, k in enumerate(group):
+            out = psend if k else precv
+            out[peer[k]] = packed[i * cap : (i + 1) * cap]
+        for k in ready:
+            copy(psend, precv, psem_s, psem_r, k).start()
+        ready = [k for k in group if k]
+    for k in ready:
+        copy(psend, precv, psem_s, psem_r, k).start()
 
     counts = jnp.sum(asked, axis=0, keepdims=True)
     counts_ref[...] = counts.astype(jnp.int32)
@@ -207,7 +204,7 @@
     entropy = jnp.sum(terms, axis=1, keepdims=True)
     flag_ref[0, 0] = jnp.max(crecv[:, 0, per:]).astype(jnp.int32)
 
-    each_peer(lambda r: arrived(psend, precv, psem_s, psem_r, r))
+    wait_all(psend, precv, psem_s, psem_r)
     packs = precv[...].reshape(n * cap, width)
     quant = jnp.dot(sel[...], packs, preferred_element_type=F32).astype(BF16)
     quant_ref[...] = quant
@@ -234,34 +231,39 @@
         lsend[p, :, :per] = sums[p : p + 1, :]
         lsend[p, :, per:] = tail
     lrecv[pl.ds(me, 1)] = lsend[pl.ds(me, 1)]
-    each_peer(lambda r: copy(lsend, lrecv, lsem_s, lsem_r, r).start())
-
-    def sent(r):
-        copy(csend, crecv, csem_s, csem_r, r).wait_send()
-        copy(psend, precv, psem_s, psem_r, r).wait_send()
-
-    each_peer(sent)
-    each_peer(lambda r: arrived(lsend, lrecv, lsem_s, lsem_r, r))
+    start_all(lsend, lrecv, lsem_s, lsem_r)
+
+    sent_all(csend, crecv, csem_s, csem_r)
+    sent_all(psend, precv, psem_s, psem_r)
+    wait_all(lsend, lrecv, lsem_s, lsem_r)
     added = jnp.sum(lrecv[:, 0, :], axis=0, keepdims=True)
     closs_ref[...] = added[:, :per]
     ends = added[:, per:]
     commit_ref[0, 0] = jnp.sum(jnp.where(lane1 == 0, ends, 0.0)) * (0.25 / total_tokens)
     perp = jnp.exp(-jnp.sum(jnp.where(lane1 == 1, ends, 0.0), axis=1, keepdims=True))
     perp_ref[0, 0] = jnp.max(jnp.broadcast_to(perp, (1, EXTRA)))
-    each_peer(lambda r: copy(lsend, lrecv, lsem_s, lsem_r, r).wait_send())
-
-
-def asked_plan(n, cols, tokens, codebook, codes):
+    sent_all(lsend, lrecv, lsem_s, lsem_r)
+
+
+def send_order(n, cols):
+    turns = sorted(range(n // cols), key=lambda d: (abs(2 * d - n // cols), d))
+    turns = [d for d in turns if d] + [0]
+    blocks = [(d, h) for d in turns for h in (0, 1)]
+    half = cols // 2
+    spread = sorted(blocks[2:-2], key=lambda b: b[1])
+    blocks = blocks[:2] + spread + [(0, 1), (0, 0)]
+    return [d * cols + h * half + c for d, h in blocks for c in range(half)]
+
+
+def exchange(n, cols, cap, number, tokens, codebook, codes):
     rows, width = tokens.shape
     per = codebook.shape[0]
-    cap = -(-2 * rows // (n * 16)) * 16
-    stride = next(s for s in range(n // 3 + 1, 2 * n) if math.gcd(s, n) == 1)
     vmem = pl.BlockSpec(memory_space=pltpu.VMEM)
     smem = pl.BlockSpec(memory_space=pltpu.SMEM)
     dma = pltpu.SemaphoreType.DMA((n,))
     message = pltpu.VMEM((n, 1, per + EXTRA), F32)
-    quantized, token_loss, counts, code_loss, commitment, perplexity, flag = pl.pallas_call(
-        functools.partial(kernel, n, cols, cap, stride),
+    return pl.pallas_call(
+        functools.partial(kernel, n, cols, cap, send_order(n, cols)),
         out_shape=(
             jax.ShapeDtypeStruct((rows, width), BF16),
             jax.ShapeDtypeStruct((1, rows), F32),
@@ -283,15 +285,31 @@
             pltpu.VMEM((rows, n * cap), BF16),
             dma, dma, dma, dma, dma, dma,
         ],
-        compiler_params=pltpu.CompilerParams(collective_id=0, has_side_effects=True),
-    )(codes.reshape(1, rows), tokens, codebook)
+        compiler_params=pltpu.CompilerParams(collective_id=number, has_side_effects=True),
+    )(codes, tokens, codebook)
+
+
+def asked_plan(n, cols, cap, tokens, codebook, codes):
+    rows = tokens.shape[0]
+    per = codebook.shape[0]
+    code_row = codes.reshape(1, rows)
+    quantized, token_loss, counts, code_loss, commitment, perplexity, flag = exchange(
+        n, cols, cap, 0, tokens, codebook, code_row
+    )
 
     def kept():
         return quantized, token_loss.reshape(rows), code_loss.reshape(per), commitment[0, 0]
 
-    quantized, token_loss, code_loss, commitment = lax.cond(
-        flag[0, 0] > cap, lambda: ring_plan(n, tokens, codebook, codes), kept
-    )
+    def wider():
+        q, t, _, c, m, _, _ = exchange(n, cols, 2 * cap, 1, tokens, codebook, code_row)
+        return q, t.reshape(rows), c.reshape(per), m[0, 0]
+
+    def any_codes():
+        return lax.cond(
+            flag[0, 0] > 2 * cap, lambda: ring_plan(n, tokens, codebook, codes), wider
+        )
+
+    quantized, token_loss, code_loss, commitment = lax.cond(flag[0, 0] > cap, any_codes, kept)
     return (
         quantized,
         token_loss,
@@ -305,19 +323,20 @@
 def on_device(n, cols, tokens, codebook, codes):
     rows, width = tokens.shape
     per = codebook.shape[0]
-    cap = -(-2 * rows // (n * 16)) * 16
+    cap = -(-rows // (n * 16)) * 16
     fits = (
         per % 128 == 0
         and per & (per - 1) == 0
         and rows % 128 == 0
         and width % 128 == 0
         and n * cap % 128 == 0
-        and n % 8 == 0
+        and cols % 8 == 0
+        and n // cols > 1
         and n <= 128
-        and cap < min(per, 256)
+        and 2 * cap < min(per, 256)
     )
     if fits:
-        return asked_plan(n, cols, tokens, codebook, codes)
+        return asked_plan(n, cols, cap, tokens, codebook, codes)
     return dense_plan(tokens, codebook, codes)
 
 

time: 51.5 us -> 44.4 us (0.86)
  Pallas kernels: 41 us -> 33.3 us
  other arithmetic: 0.02 us -> 0.61 us
    pallas_call x1, Pallas kernels: 41 us -> 33.3 us  [exchange(): pl.pallas_call(functools.partial(kernel, n, cols, cap, send_order(n, cols...]
    another operation x1, other arithmetic: 0.02 us -> 0.61 us
    reshape x1, local copies, waits for them, and re-layouts: 0.58 us -> 0.01 us  [asked_plan(): code_row = codes.reshape(1, rows)]
    unnamed x11 -> x9, local copies, waits for them, and re-layouts: 4.85 us -> 5.3 us
where the time goes in v2:
time: 44.4 us; the launch traced here: 44.2 us
  Pallas kernels  33.3 us (75%)
  local copies, waits for them, and re-layouts  5.3 us (12%)
  between operations  4.9 us (11%)
  other arithmetic  0.61 us (1%)
    pallas_call x1, Pallas kernels, exchange(): pl.pallas_call(functools.partial(kernel, n, cols, cap, send_order(n, cols...  33.3 us
    unnamed x9, local copies, waits for them, and re-layouts  5.3 us

profile of v2, /device:TPU:0, one launch (start us, length us, event | category | flops | bytes accessed | tf_op | source)
XLA Modules:
  0.0 44.2 jit_solution(15242491422312314159)
XLA Ops:
  0.6 0.0 copy-start
  0.6 0.7 %copy.61 = s32[768]{0:T(1024)S(1)} copy(s32[768]{0:T(1024)} %param.13) | data formatting | bytes 6144
  1.4 0.9 %copy.60.book_ref = bf16[512,256]{1,0:T(8,128)(2,1)S(1)} copy(bf16[512,256]{1,0:T(8,128)(2,1)} %param.12) | data formatting | bytes 524288
  2.3 0.0 copy-done
  2.3 33.3 %shard_map.82 = (bf16[768,256]{1,0:T(8,128)(2,1)}, f32[1,768]{1,0:T(1,128)S(1)}, s32[1,512]{1,0:T(1,128)}, f32[1,512]{1,0:T(1,128)}, f32[1,1]{1,0:T(1,128)}, /*index=5*/f32[1,1]{1,0:T(1,128)}, s32[1,1]{1,0:T(1,128)}) custom-call(s32[1,768]{1,0:T(1,128)S(1)} %reshape.65.codes_ref, bf16[768,256]{1,0:T(8,128)(2,1)S(1)} %copy-done, ...), custom_call_target="tpu_custom_call" | custom-call | tf_op jit(solution)/shard_map/pallas_call | solution.py:265
  36.4 0.6 %conditional.2 = ((bf16[768,256]{1,0:T(8,128)(2,1)}, f32[768]{0:T(1024)}, f32[512]{0:T(512)}, f32[]{:T(128)})) conditional(s32[]{:T(128)} %bitcast.6, (f32[1,768]{1,0:T(1,128)S(1)}, f32[1,512]{1,0:T(1,128)}, f32[1,1]{1,0:T(1,128)}, bf16[768,256]{1,0:T(8,128)(2,1)}) %tuple.99, (s32[1,1]{1,0:T(1,128)}, s32[1,768]{1,0:T(1,128)S(1)}, ...), branch_computations={%region_0.0_spmd, %region_1.12_spmd} | conditional | flops 1619264 | bytes 4443314 | solution.py:312
  36.4 0.6 %reduce = f32[768]{0:T(1024)} reduce(f32[1,768]{1,0:T(1,128)S(1)} %get-tuple-element.281, f32[]{:T(128)} %constant.216), dimensions={0}, to_apply=%get-tuple-element.281.reduce_sub_computation | reduce | bytes 6148 | tf_op jit(solution)/shard_map
  37.0 0.0 copy-start.2
  37.0 1.8 %copy.62 = bf16[768,256]{1,0:T(8,128)(2,1)} copy(bf16[768,256]{1,0:T(8,128)(2,1)} %get-tuple-element.563) | data formatting | bytes 786432
  38.8 0.0 copy-done.2
  38.8 0.6 %copy.63 = s32[512]{0:T(512)} copy(s32[512]{0:T(512)S(1)} %bitcast.11) | data formatting | bytes 4096
  39.3 1.3 %copy.64 = f32[512]{0:T(512)} copy(f32[512]{0:T(512)} %get-tuple-element.566) | data formatting | bytes 4096
  (1 shorter events, 0.0 us)
Async XLA Ops:
  0.6 1.7 %copy-start = (bf16[768,256]{1,0:T(8,128)(2,1)S(1)}, bf16[768,256]{1,0:T(8,128)(2,1)}, u32[]{:S(2)}) copy-start(bf16[768,256]{1,0:T(8,128)(2,1)} %tokens_ref.1) | copy-start | bytes 1179652
  37.0 1.8 %copy-start.2 = (s32[1,512]{1,0:T(1,128)S(1)}, s32[1,512]{1,0:T(1,128)}, u32[]{:S(2)}) copy-start(s32[1,512]{1,0:T(1,128)} %get-tuple-element.340) | copy-start | bytes 6148

commit v3 on v2

--- a/solution.py
+++ b/solution.py
@@ -134,7 +134,7 @@
                 barrier, inc=1, device_id=at[k], device_id_type=pl.DeviceIdType.MESH
             )
 
-    code_row = codes_ref[...]
+    code_row = codes_ref[...].reshape(1, rows)
     hi_row = lax.shift_right_logical(code_row, bits)
     code_col = jnp.broadcast_to(code_row.astype(F32), (128, rows)).T.astype(jnp.int32)
     hi_col = lax.shift_right_logical(code_col, bits)
@@ -196,7 +196,7 @@
         copy(psend, precv, psem_s, psem_r, k).start()
 
     counts = jnp.sum(asked, axis=0, keepdims=True)
-    counts_ref[...] = counts.astype(jnp.int32)
+    counts_ref[...] = counts.astype(jnp.int32).reshape(per)
     probs = counts / total_tokens
     terms = jnp.where(
         counts > 0.5, probs * jnp.log(jnp.maximum(probs, 1.0 / total_tokens)), 0.0
@@ -214,7 +214,7 @@
     for k in range(1, width // 128):
         folded = folded + square[:, k * 128 : (k + 1) * 128]
     tloss = jnp.sum(folded.T, axis=0, keepdims=True) / width
-    tloss_ref[...] = tloss
+    tloss_ref[...] = tloss.reshape(rows)
     part = jnp.sum(tloss, axis=1, keepdims=True)
 
     first = tloss.astype(BF16).astype(F32)
@@ -237,7 +237,7 @@
     sent_all(psend, precv, psem_s, psem_r)
     wait_all(lsend, lrecv, lsem_s, lsem_r)
     added = jnp.sum(lrecv[:, 0, :], axis=0, keepdims=True)
-    closs_ref[...] = added[:, :per]
+    closs_ref[...] = added[:, :per].reshape(per)
     ends = added[:, per:]
     commit_ref[0, 0] = jnp.sum(jnp.where(lane1 == 0, ends, 0.0)) * (0.25 / total_tokens)
     perp = jnp.exp(-jnp.sum(jnp.where(lane1 == 1, ends, 0.0), axis=1, keepdims=True))
@@ -266,9 +266,9 @@
         functools.partial(kernel, n, cols, cap, send_order(n, cols)),
         out_shape=(
             jax.ShapeDtypeStruct((rows, width), BF16),
-            jax.ShapeDtypeStruct((1, rows), F32),
-            jax.ShapeDtypeStruct((1, per), jnp.int32),
-            jax.ShapeDtypeStruct((1, per), F32),
+            jax.ShapeDtypeStruct((rows,), F32),
+            jax.ShapeDtypeStruct((per,), jnp.int32),
+            jax.ShapeDtypeStruct((per,), F32),
             jax.ShapeDtypeStruct((1, 1), F32),
             jax.ShapeDtypeStruct((1, 1), F32),
             jax.ShapeDtypeStruct((1, 1), jnp.int32),
@@ -292,17 +292,16 @@
 def asked_plan(n, cols, cap, tokens, codebook, codes):
     rows = tokens.shape[0]
     per = codebook.shape[0]
-    code_row = codes.reshape(1, rows)
     quantized, token_loss, counts, code_loss, commitment, perplexity, flag = exchange(
-        n, cols, cap, 0, tokens, codebook, code_row
+        n, cols, cap, 0, tokens, codebook, codes
     )
 
     def kept():
-        return quantized, token_loss.reshape(rows), code_loss.reshape(per), commitment[0, 0]
+        return quantized, token_loss, code_loss, commitment[0, 0]
 
     def wider():
-        q, t, _, c, m, _, _ = exchange(n, cols, 2 * cap, 1, tokens, codebook, code_row)
-        return q, t.reshape(rows), c.reshape(per), m[0, 0]
+        q, t, _, c, m, _, _ = exchange(n, cols, 2 * cap, 1, tokens, codebook, codes)
+        return q, t, c, m[0, 0]
 
     def any_codes():
         return lax.cond(
@@ -313,7 +312,7 @@
     return (
         quantized,
         token_loss,
-        counts.reshape(per),
+        counts,
         code_loss,
         commitment,
         perplexity[0, 0],

time: 44.4 us -> 45.2 us (1.018)
  local copies, waits for them, and re-layouts: 5.3 us -> 6.55 us
  other arithmetic: 0.61 us -> 0 us
    unnamed x9 -> x10, local copies, waits for them, and re-layouts: 5.3 us -> 6.55 us
    another operation x1 -> x0, other arithmetic: 0.61 us -> none
where the time goes in v3:
time: 45.2 us; the launch traced here: 44.9 us
  Pallas kernels  33.3 us (74%)
  local copies, waits for them, and re-layouts  6.55 us (14%)
  between operations  4.81 us (11%)
    pallas_call x1, Pallas kernels, exchange(): pl.pallas_call(functools.partial(kernel, n, cols, cap, send_order(n, cols...  33.3 us
    unnamed x10, local copies, waits for them, and re-layouts  6.55 us

profile of v3, /device:TPU:0, one launch (start us, length us, event | category | flops | bytes accessed | tf_op | source)
XLA Modules:
  0.0 44.9 jit_solution(6851795201340870674)
XLA Ops:
  0.6 0.0 copy-start
  0.6 0.7 %copy.61.codes_ref = s32[768]{0:T(1024)S(1)} copy(s32[768]{0:T(1024)} %param.13) | data formatting | bytes 6144
  1.4 0.9 %copy.60.book_ref = bf16[512,256]{1,0:T(8,128)(2,1)S(1)} copy(bf16[512,256]{1,0:T(8,128)(2,1)} %param.12) | data formatting | bytes 524288
  2.3 0.0 copy-done
  2.3 33.3 %shard_map.82 = (bf16[768,256]{1,0:T(8,128)(2,1)}, f32[768]{0:T(1024)}, s32[512]{0:T(512)}, f32[512]{0:T(512)}, f32[1,1]{1,0:T(1,128)}, /*index=5*/f32[1,1]{1,0:T(1,128)}, s32[1,1]{1,0:T(1,128)}) custom-call(s32[768]{0:T(1024)S(1)} %copy.61.codes_ref, bf16[768,256]{1,0:T(8,128)(2,1)S(1)} %copy-done, bf16[512,256]{1,0:T(8,128)(2,1)S(1)} %copy.60.book_ref), custom_call_target="tpu_custom_call" | custom-call | tf_op jit(solution)/shard_map/pallas_call | solution.py:265
  36.2 0.2 conditional.2
  36.4 1.8 %copy.62 = bf16[768,256]{1,0:T(8,128)(2,1)} copy(bf16[768,256]{1,0:T(8,128)(2,1)} %get-tuple-element.560) | data formatting | bytes 786432
  38.2 0.0 copy-start.1
  38.2 1.3 %copy.63 = f32[768]{0:T(1024)} copy(f32[768]{0:T(1024)} %get-tuple-element.561) | data formatting | bytes 6144
  39.5 0.0 copy-done.1
  39.5 0.6 %copy.64 = s32[512]{0:T(512)} copy(s32[512]{0:T(512)S(1)} %copy-done.1) | data formatting | bytes 4096
  40.0 1.2 %copy.65 = f32[512]{0:T(512)} copy(f32[512]{0:T(512)} %get-tuple-element.563) | data formatting | bytes 4096
Async XLA Ops:
  0.6 1.7 %copy-start = (bf16[768,256]{1,0:T(8,128)(2,1)S(1)}, bf16[768,256]{1,0:T(8,128)(2,1)}, u32[]{:S(2)}) copy-start(bf16[768,256]{1,0:T(8,128)(2,1)} %tokens_ref.1) | copy-start | bytes 1179652
  38.2 1.3 %copy-start.1 = (s32[512]{0:T(512)S(1)}, s32[512]{0:T(512)}, u32[]{:S(2)}) copy-start(s32[512]{0:T(512)} %get-tuple-element.562) | copy-start | bytes 6148
